TPU v7x, 128 devices: a whole 4x4x4 slice. The times are simulated.
128 devices in a mesh: dp: 1, tp: 2 (over core), sp: 64 (over z, y, x).
Axes of the slice: x: 4, y: 4, z: 4, core: 2. Of those that a mesh axis runs over, the one named last changes fastest.
Arguments:
- tok_emb: bfloat16 [4, 32, 2048], P(None, 'dp')
- lengths: int32 [32], P('dp')
- key_cache: bfloat16 [2, 32, 8192, 2, 128], P(None, 'dp', 'sp', 'tp')
- val_cache: bfloat16 [2, 32, 8192, 2, 128], P(None, 'dp', 'sp', 'tp')
- gain_attn: bfloat16 [2, 2048], replicated
- gain_mlp: bfloat16 [2, 2048], replicated
- w_query: bfloat16 [2, 2048, 2048], P(None, None, 'tp')
- w_key: bfloat16 [2, 2048, 256], P(None, None, 'tp')
- w_value: bfloat16 [2, 2048, 256], P(None, None, 'tp')
- w_out: bfloat16 [2, 2048, 2048], P(None, 'tp')
- w_gate: bfloat16 [2, 2048, 11008], P(None, None, 'tp')
- w_up: bfloat16 [2, 2048, 11008], P(None, None, 'tp')
- w_down: bfloat16 [2, 11008, 2048], P(None, 'tp')
Outputs:
- output 1: bfloat16 [4, 32, 2048], P(None, 'dp')
- output 2: bfloat16 [2, 32, 8192, 2, 128], P(None, 'dp', 'sp', 'tp')
- output 3: bfloat16 [2, 32, 8192, 2, 128], P(None, 'dp', 'sp', 'tp')
All inputs are finite; a program needn't handle non-finite values.
Results may differ from a plain program's by a relative error of at most 0.0153106.
Values sent between devices are 32-bit elements.
A program may use at most 1 GiB of HBM per device.

v0:
```python
import jax
import jax.numpy as jnp
from jax import lax
from jax.sharding import PartitionSpec as P

EPS = 1e-5
ROPE_BASE = 500000.0


def rms_norm(hidden, gain_vec):
    x_float = hidden.astype(jnp.float32)
    inv_rms = lax.rsqrt(jnp.mean(x_float * x_float, axis=-1, keepdims=True) + EPS)
    return (x_float * inv_rms * gain_vec.astype(jnp.float32)).astype(jnp.bfloat16)


def rotary(in_vecs, positions):
    head_dim = in_vecs.shape[-1]
    half_dim = head_dim // 2
    inv_freq = 1.0 / (ROPE_BASE ** (jnp.arange(half_dim).astype(jnp.float32) * 2.0 / head_dim))
    angles = positions.astype(jnp.float32)[:, None] * inv_freq[None, :]
    cos_a = jnp.cos(angles)[:, None, :]
    sin_a = jnp.sin(angles)[:, None, :]
    front_half = in_vecs[..., :half_dim]
    back_half = in_vecs[..., half_dim:]
    return jnp.concatenate([front_half * cos_a - back_half * sin_a, back_half * cos_a + front_half * sin_a], axis=-1)


def project(normed, weight):
    return jnp.dot(normed, weight, preferred_element_type=jnp.float32)


def solution(mesh):
    sp_size = mesh.shape['sp']

    def local_fn(tok_emb, lengths, key_cache, val_cache, gain_attn, gain_mlp, w_query, w_key, w_value, w_out, w_gate, w_up, w_down):
        n_steps, n_batch, width = tok_emb.shape
        n_layers, _, loc_len, kv_loc, head_dim = key_cache.shape
        heads_loc = w_query.shape[2] // head_dim
        group_size = heads_loc // kv_loc
        n_tok = n_steps * n_batch
        my_sp = lax.axis_index('sp')
        slot_pos = jnp.arange(loc_len) * sp_size + my_sp
        cur_pos = lengths[:, None] + jnp.arange(n_steps)[None, :]
        tok_pos = cur_pos.reshape(n_tok)
        write_slot = jnp.where(cur_pos % sp_size == my_sp, cur_pos // sp_size, loc_len)
        valid_mask = (slot_pos[None, None, :] <= cur_pos[:, :, None])[:, None, :, None, :]
        row_ids = jnp.arange(n_batch)[:, None]
        new_keys = key_cache
        new_vals = val_cache
        hidden = jnp.swapaxes(tok_emb, 0, 1).reshape(n_tok, width)
        for layer_idx in range(n_layers):
            normed = rms_norm(hidden, gain_attn[layer_idx])
            q_vec = project(normed, w_query[layer_idx]).reshape(n_tok, heads_loc, head_dim)
            k_vec = project(normed, w_key[layer_idx]).reshape(n_tok, kv_loc, head_dim)
            v_vec = project(normed, w_value[layer_idx]).astype(jnp.bfloat16)
            q_rot = rotary(q_vec, tok_pos).astype(jnp.bfloat16).reshape(n_batch, n_steps, kv_loc, group_size, head_dim)
            k_rot = rotary(k_vec, tok_pos).astype(jnp.bfloat16).reshape(n_batch, n_steps, kv_loc, head_dim)
            new_keys = new_keys.at[layer_idx, row_ids, write_slot].set(k_rot, mode='drop')
            new_vals = new_vals.at[layer_idx, row_ids, write_slot].set(v_vec.reshape(n_batch, n_steps, kv_loc, head_dim), mode='drop')
            scores = jnp.einsum('bskgd,bjkd->bksgj', q_rot, new_keys[layer_idx], preferred_element_type=jnp.float32) * head_dim ** -0.5
            scores = jnp.where(valid_mask, scores, -1e30)
            loc_max = jnp.max(scores, axis=-1, keepdims=True)
            prob_w = jnp.exp(scores - loc_max)
            loc_sum = jnp.sum(prob_w, axis=-1, keepdims=True)
            loc_out = jnp.einsum('bksgj,bjkd->bksgd', prob_w.astype(jnp.bfloat16), new_vals[layer_idx], preferred_element_type=jnp.float32)
            glob_max = lax.pmax(loc_max, 'sp')
            rescale = jnp.exp(loc_max - glob_max)
            merged = lax.psum(jnp.concatenate([loc_out, loc_sum], axis=-1) * rescale, 'sp')
            attn_out = (merged[..., :head_dim] / merged[..., head_dim:]).astype(jnp.bfloat16)
            attn_out = jnp.swapaxes(attn_out, 1, 2).reshape(n_tok, heads_loc * head_dim)
            proj_sum = lax.psum(project(attn_out, w_out[layer_idx]), 'tp')
            hidden = (hidden.astype(jnp.float32) + proj_sum).astype(jnp.bfloat16)
            normed = rms_norm(hidden, gain_mlp[layer_idx])
            mlp_act = (jax.nn.silu(project(normed, w_gate[layer_idx])) * project(normed, w_up[layer_idx])).astype(jnp.bfloat16)
            down_sum = lax.psum(project(mlp_act, w_down[layer_idx]), 'tp')
            hidden = (hidden.astype(jnp.float32) + down_sum).astype(jnp.bfloat16)
        hidden = jnp.swapaxes(hidden.reshape(n_batch, n_steps, width), 0, 1)
        return hidden, new_keys, new_vals

    cache_spec = P(None, 'dp', 'sp', 'tp', None)
    col_spec = P(None, None, 'tp')
    row_spec = P(None, 'tp', None)
    emb_spec = P(None, 'dp', None)
    return jax.shard_map(local_fn, mesh=mesh, in_specs=(emb_spec, P('dp'), cache_spec, cache_spec, P(), P(), col_spec, col_spec, col_spec, row_spec, col_spec, col_spec, row_spec), out_specs=(emb_spec, cache_spec, cache_spec), check_vma=False)
```

profile of v0, /device:TPU:1, one launch (start us, length us, event | category | flops | bytes accessed | tf_op | source)
XLA Modules:
  0.0 1228.2 jit_solution(8457309703477068068)
XLA Ops:
  7.2 1.5 copy-done.5
  12.7 5.9 slice_bitcast_fusion
  18.6 6.5 copy.51
  25.1 3.6 fusion.124
  30.9 8.7 scatter_fusion
  39.6 13.8 %scatter_fusion.1 = bf16[2,32,128,128]{3,2,1,0:T(8,128)(2,1)} fusion(bf16[2,32,128,128]{3,2,1,0:T(8,128)(2,1)} %bitcast.163, s32[128]{0:T(128)S(1)} %reshape.597, bf16[128,128]{1,0:T(8,128)(2,1)S(1)} %convolution_convert_fusion.1), kind=kCustom, calls=%fused_computation.1 | custom fusion | bytes 99840 | tf_op jit(solution)/shard_map/scatter | solution.py:59
  56.2 296.4 %pmax.14 = f32[32,1,4,8,1]{3,2,0,4,1:T(4,128)S(1)} all-reduce(f32[32,1,4,8,1]{3,2,0,4,1:T(4,128)S(1)} %bitcast.166), channel_id=1, replica_groups=mesh['dp'=1,'tp'=2,'sp'=64] {'sp'}, use_global_device_ids=true, to_apply=%region_5.6 | all-reduce | flops 1024 | bytes 8192 | tf_op jit(solution)/shard_map/pmax | solution.py:66
  353.5 2.2 maximum_multiply_fusion
  355.8 177.6 %all-reduce.7.cloned.1.call-done = f32[32,1,4,8,129]{4,3,2,0,1:T(8,128)} async-done(((f32[32,1,4,8,129]{4,3,2,0,1:T(8,128)}), f32[32,1,4,8,129]{4,3,2,0,1:T(8,128)}) %all-reduce.7.cloned.1.call-update) | async-done | bytes 528400 | tf_op jit(solution)/shard_map/psum | solution.py:68
  536.1 3.9 fusion.32
  540.4 1.6 copy.49
  542.1 1.6 reshape.588
  543.7 20.8 %all-reduce.9.cloned.1.call-done = f32[128,2048]{1,0:T(8,128)} async-done(((f32[128,2048]{1,0:T(8,128)}), f32[128,2048]{1,0:T(8,128)}) %all-reduce.9.cloned.1.call-update) | async-done | bytes 1048592 | tf_op jit(solution)/shard_map/psum | solution.py:71
  566.0 9.4 fusion.10
  575.4 9.5 fusion.27
  584.9 10.2 fusion.6
  595.2 6.6 copy.60
  601.9 19.4 %all-reduce.11.cloned.1.call-done = f32[128,2048]{1,0:T(8,128)} async-done(((f32[128,2048]{1,0:T(8,128)}), f32[128,2048]{1,0:T(8,128)}) %all-reduce.11.cloned.1.call-update) | async-done | bytes 1048592 | tf_op jit(solution)/shard_map/psum | solution.py:75
  621.3 1.6 fusion.42
  628.8 8.7 scatter_fusion.2
  637.6 2.0 fusion.123
  639.5 294.0 %pmax.15 = f32[32,1,4,8,1]{3,2,0,4,1:T(4,128)S(1)} all-reduce(f32[32,1,4,8,1]{3,2,0,4,1:T(4,128)S(1)} %bitcast.165), channel_id=1, replica_groups=mesh['dp'=1,'tp'=2,'sp'=64] {'sp'}, use_global_device_ids=true, to_apply=%region_15.16 | all-reduce | flops 1024 | bytes 8192 | tf_op jit(solution)/shard_map/pmax | solution.py:66
  933.6 13.8 %scatter_fusion.3 = bf16[2,32,128,128]{3,2,1,0:T(8,128)(2,1)} fusion(bf16[2,32,128,128]{3,2,1,0:T(8,128)(2,1)} %scatter_fusion.1, s32[128]{0:T(128)S(1)} %reshape.617, bf16[128,128]{1,0:T(8,128)(2,1)S(1)} %convolution_convert_fusion), kind=kCustom, calls=%fused_computation.3 | custom fusion | bytes 99840 | tf_op jit(solution)/shard_map/scatter | solution.py:59
  947.8 2.5 convolution_bitcast_fusion
  951.1 2.3 maximum_multiply_fusion.1
  953.5 177.5 %all-reduce.13.cloned.1.call-done = f32[32,1,4,8,129]{4,3,2,0,1:T(8,128)} async-done(((f32[32,1,4,8,129]{4,3,2,0,1:T(8,128)}), f32[32,1,4,8,129]{4,3,2,0,1:T(8,128)}) %all-reduce.13.cloned.1.call-update) | async-done | bytes 528400 | tf_op jit(solution)/shard_map/psum | solution.py:68
  1133.8 3.9 fusion.30
  1137.8 24.4 %all-reduce.15.cloned.1.call-done = f32[128,2048]{1,0:T(8,128)} async-done(((f32[128,2048]{1,0:T(8,128)}), f32[128,2048]{1,0:T(8,128)}) %all-reduce.15.cloned.1.call-update) | async-done | bytes 1048592 | tf_op jit(solution)/shard_map/psum | solution.py:71
  1163.7 9.2 fusion.4
  1172.9 9.5 fusion.24
  1182.3 10.2 fusion
  1192.6 26.1 %all-reduce.17.cloned.1.call-done = f32[128,2048]{1,0:T(8,128)} async-done(((f32[128,2048]{1,0:T(8,128)}), f32[128,2048]{1,0:T(8,128)}) %all-reduce.17.cloned.1.call-update) | async-done | bytes 1048592 | tf_op jit(solution)/shard_map/psum | solution.py:75
  (99 shorter events, 28.7 us)
Async XLA Ops:
  7.2 1.6 copy-start.5
  7.2 526.2 %all-reduce.7.cloned.1.call-start = ((), (), s32[]{:S(2)}) async-start(), calls=%async_computation | async-start | bytes 2097152 | tf_op jit(solution)/shard_map/psum | solution.py:68
  8.8 1.3 copy-start.10
  8.8 1.4 copy-start.3
  10.1 1.2 copy-start.12
  10.1 1.5 copy-start.9
  11.1 7.5 copy-start.6
  25.1 5.8 copy-start.2
  53.4 1.6 copy-start.4
  355.7 208.8 %all-reduce.9.cloned.1.call-start = ((), (), s32[]{:S(2)}) async-start(), calls=%async_computation.1 | async-start | bytes 2097152 | tf_op jit(solution)/shard_map/psum | solution.py:71
  540.1 3.6 copy-start.11
  540.1 81.1 %all-reduce.11.cloned.1.call-start = ((), (), s32[]{:S(2)}) async-start(), calls=%async_computation.2 | async-start | bytes 2097152 | tf_op jit(solution)/shard_map/psum | solution.py:75
  566.0 9.4 copy-start.7
  595.1 535.9 %all-reduce.13.cloned.1.call-start = ((), (), s32[]{:S(2)}) async-start(), calls=%async_computation.3 | async-start | bytes 2097152 | tf_op jit(solution)/shard_map/psum | solution.py:68
  595.2 26.1 %copy-start.8 = (bf16[128,2048]{1,0:T(8,128)(2,1)S(1)}, bf16[128,2048]{1,0:T(8,128)(2,1)}, u32[]{:S(2)}) copy-start(bf16[128,2048]{1,0:T(8,128)(2,1)} %copy-done.7) | copy-start | bytes 1572868
  621.3 4.5 copy-start
  637.6 312.8 %copy-start.1 = (bf16[2,32,128,128]{3,2,1,0:T(8,128)(2,1)}, bf16[2,32,128,128]{3,2,1,0:T(8,128)(2,1)S(1)}, u32[]{:S(2)}) copy-start(bf16[2,32,128,128]{3,2,1,0:T(8,128)(2,1)S(1)} %scatter_fusion.2) | copy-start | bytes 6291460
  953.4 208.8 %all-reduce.15.cloned.1.call-start = ((), (), s32[]{:S(2)}) async-start(), calls=%async_computation.4 | async-start | bytes 2097152 | tf_op jit(solution)/shard_map/psum | solution.py:71
  1137.8 81.0 %all-reduce.17.cloned.1.call-start = ((), (), s32[]{:S(2)}) async-start(), calls=%async_computation.5 | async-start | bytes 2097152 | tf_op jit(solution)/shard_map/psum | solution.py:75
Sparse Core Ops, SparseCore 0:
  355.8 177.4 all-reduce.6
  540.2 24.2 all-reduce.8
  595.2 25.9 all-reduce.10
  953.6 177.4 all-reduce.12
  1137.9 24.2 all-reduce.14
  1192.7 25.9 all-reduce.16
where the time goes:
time: 1230 us
  blocking collectives  590 us (48%)
  waiting for transfers between devices  446 us (36%)
  matrix products  81.9 us (7%)
  local copies, waits for them, and re-layouts  79.4 us (6%)
  other arithmetic  15.6 us (1%)
  between operations  14.6 us (1%)
    pmax x2, blocking collectives, local_fn(): glob_max = lax.pmax(loc_max, 'sp')  590 us
    psum x2, waiting for transfers between devices, local_fn(): lax.psum(jnp.concatenate([loc_out, loc_sum], axis=-1) * rescale, 'sp')  355 us
    dot_general x14, matrix products, project(): return jnp.dot(normed, weight, preferred_element_type=jnp.float32)  75.4 us
    psum x2, waiting for transfers between devices, local_fn(): down_sum = lax.psum(project(mlp_act, w_down[layer_idx]), 'tp')  45.5 us
    psum x2, waiting for transfers between devices, local_fn(): proj_sum = lax.psum(project(attn_out, w_out[layer_idx]), 'tp')  45.2 us
    scatter x2, local copies, waits for them, and re-layouts, local_fn(): new_vals.at[layer_idx, row_ids, write_slot]  27.6 us
  transfers between devices with their start and end apart: 6, of which 6 were waited for; matrix products, arithmetic and copies ran while one was open for 1% of the time, Pallas kernels for 0%

commit v1 on v0

v1 whole, which is shorter than its diff:
```python
import functools

import jax
import jax.numpy as jnp
from jax import lax
from jax.experimental import pallas as pl
from jax.experimental.pallas import tpu as pltpu
from jax.sharding import PartitionSpec as P

EPS = 1e-5
ROPE_BASE = 500000.0
CHUNK = 512
SLOTS = 6
UNROLL = 8
F32 = jnp.float32
BF16 = jnp.bfloat16
MESH = pl.DeviceIdType.MESH


def dot(a, b):
    return jnp.dot(a, b, preferred_element_type=F32)


def norm(u, gain):
    inv = lax.rsqrt(jnp.mean(u * u, axis=-1, keepdims=True) + EPS)
    return (u * inv * gain).astype(BF16)


def iota(shape, dim):
    return lax.broadcasted_iota(jnp.int32, shape, dim)


def kernel(sp, n_steps, n_batch, side,
           len_ref, freq_ref, ga_ref, gm_ref, x_hbm, kc_hbm, vc_hbm, wq_hbm, wk_hbm, wv_hbm, wo_hbm, wg_hbm, wu_hbm, wd_hbm,
           hid_hbm, ko_hbm, vo_hbm,
           x_v, xn_v, wqkv_v, wo_v, kc_v, vc_v, wg_v, wu_v, wd_v, q0_v, k0_v, v0_v,
           q_recv, kv_recv, o_send, o_recv, st_send, st_recv, x_send, x_recv, acc_v, q_send, kv_send, h_send,
           h_recv, h_other, out_v, tr_v, at_v,
           in_sem, cache_sem, out_sem, wqkv_sem, wo_sem, slot_sem,
           o_ssem, o_rsem, st_ssem, st_rsem, x_ssem, x_rsem, ag_ssem, ag_rsem):
    me = lax.axis_index('sp')
    core = lax.axis_index('tp')
    n_tok = n_steps * n_batch
    width = x_v.shape[1]
    d = 128
    ff = wg_hbm.shape[2]
    heads = wq_hbm.shape[2] // d
    qw = heads * d
    n_chunks = -(-ff // CHUNK)
    total = 2 * n_chunks
    last = sp - 1
    partner = {'tp': 1 - core}

    def local(src, dst, sem):
        return pltpu.make_async_copy(src, dst, sem)

    def remote(src, dst, ssem, rsem, dev):
        return pltpu.make_async_remote_copy(src_ref=src, dst_ref=dst, send_sem=ssem, recv_sem=rsem, device_id=dev, device_id_type=MESH)

    def qkv_copies(lay):
        return (local(wq_hbm.at[lay], wqkv_v.at[:, pl.ds(0, qw)], wqkv_sem.at[0]),
                local(wk_hbm.at[lay], wqkv_v.at[:, pl.ds(qw, d)], wqkv_sem.at[1]),
                local(wv_hbm.at[lay], wqkv_v.at[:, pl.ds(qw + d, d)], wqkv_sem.at[2]))

    def chunk_copy(step, which):
        lay = step // n_chunks
        col = pl.multiple_of(jnp.minimum((step % n_chunks) * CHUNK, ff - CHUNK), d)
        slot = step % SLOTS
        if which == 2:
            return local(wd_hbm.at[lay, pl.ds(col, CHUNK), :], wd_v.at[slot], slot_sem.at[slot, 2])
        src, dst = ((wg_hbm, wg_v), (wu_hbm, wu_v))[which]
        return local(src.at[lay, :, pl.ds(col, CHUNK)], dst.at[slot], slot_sem.at[slot, which])

    x_copy = local(x_hbm, x_v, in_sem.at[0])
    x_copy.start()
    for copy in qkv_copies(0):
        copy.start()
    barrier = pltpu.get_barrier_semaphore()

    def greet(i, carry):
        pl.semaphore_signal(barrier, inc=1, device_id={'sp': lax.rem(me + i, sp)}, device_id_type=MESH)
        return carry
    lax.fori_loop(1, sp, greet, 0)
    pl.semaphore_signal(barrier, inc=1, device_id=partner, device_id_type=MESH)

    lane = iota((1, d), 1)
    sign = jnp.where(lane < d // 2, -1.0, 1.0).astype(F32)
    freq = freq_ref[...]
    brow = iota((n_batch, d), 0)

    def place(b, acc):
        return jnp.where(brow == b, len_ref[b], acc)
    pos_b = lax.fori_loop(0, n_batch, place, jnp.zeros((n_batch, d), jnp.int32))
    angles = jnp.concatenate([(pos_b + s).astype(F32) * freq for s in range(n_steps)], axis=0)
    cos_t = jnp.cos(angles)
    sin_t = jnp.sin(angles) * sign
    row16 = iota((16, d), 0)
    my_pos = len_ref[me // 2] + 2 * lax.rem(me, 2) + row16 // 8
    my_angles = my_pos.astype(F32) * freq
    my_cos = jnp.cos(my_angles)
    my_sin = jnp.sin(my_angles) * sign

    def rope(v, c, s):
        return v * c + pltpu.roll(v, d // 2, 1) * s

    def rounded(v):
        return v.astype(BF16).astype(F32)

    x_copy.wait()
    xn_v[...] = norm(x_v[...].astype(F32), ga_ref[pl.ds(0, 1), :].astype(F32))
    for copy in qkv_copies(0):
        copy.wait()
    for lay in range(2):
        local(kc_hbm.at[lay], kc_v.at[lay], cache_sem.at[lay]).start()
        local(vc_hbm.at[lay], vc_v.at[lay], cache_sem.at[2 + lay]).start()
    wo_copy = local(wo_hbm.at[0], wo_v, wo_sem.at[0])
    wo_copy.start()

    def prefetch(step, carry):
        for which in range(3):
            chunk_copy(step, which).start()
        return carry
    lax.fori_loop(0, SLOTS, prefetch, 0)

    xn = xn_v[...]
    for pair in range(heads // 2):
        both = dot(xn, wqkv_v[:, pair * 256:pair * 256 + 256])
        for g in (2 * pair, 2 * pair + 1):
            off = (g % 2) * d
            q = rounded(rope(both[:, off:off + d], cos_t, sin_t))
            for s in range(n_steps):
                q0_v[pl.ds(s * heads + g, n_batch, stride=n_steps * heads), :] = q[s * n_batch:(s + 1) * n_batch]
    both = dot(xn, wqkv_v[:, qw:qw + 256])
    k0_v[...] = rounded(rope(both[:, :d], cos_t, sin_t))
    v0_v[...] = rounded(both[:, d:])
    for copy in qkv_copies(1):
        copy.start()

    own_row = (2 * lax.rem(me, 2) + iota((16, n_tok), 0) // 8) * n_batch + me // 2
    pick = jnp.where(iota((16, n_tok), 1) == own_row, 1.0, 0.0).astype(BF16)
    u = dot(pick, x_v[...])

    pos_row = iota((32, d), 1) * sp + me - iota((32, d), 0) // heads
    lane32 = iota((32, d), 1)
    slot_rows = iota((d, d), 0).astype(F32).astype(BF16)

    def attention(lay, q_ref, new_rows):
        def group(step, stat):
            for uu in range(UNROLL):
                b = lax.rem(me // 2 + step * UNROLL + uu, n_batch)
                length = len_ref[b]
                ahead = lax.rem(me - length + 1024 * sp, sp)
                slot = jnp.where(ahead < n_steps, (length + ahead) // sp, -1)
                hit = slot_rows == jnp.full((d, d), slot.astype(F32)).astype(BF16)
                k_row, v_row = new_rows(b, jnp.minimum(ahead, n_steps - 1))
                k_new = jnp.where(hit, jnp.broadcast_to(k_row, (d, d)).astype(BF16), kc_v[lay, b])
                v_new = jnp.where(hit, jnp.broadcast_to(v_row, (d, d)).astype(BF16), vc_v[lay, b])
                kc_v[lay, b] = k_new
                vc_v[lay, b] = v_new
                rows = pl.ds(pl.multiple_of(b * 32, 32), 32)
                q = q_ref[rows, :].astype(BF16)
                s = lax.dot_general(q, k_new, (((1,), (1,)), ((), ())), preferred_element_type=F32) * (d ** -0.5)
                s = jnp.where(pos_row <= length, s, -1e30)
                m = jnp.max(s, axis=-1, keepdims=True)
                w = jnp.exp(s - m)
                l = jnp.sum(w, axis=-1, keepdims=True)
                o_send[rows, :] = dot(w.astype(BF16), v_new)
                stat = jnp.where(lane32 == b, m, jnp.where(lane32 == 64 + b, l, stat))
            for uu in range(2 * UNROLL):
                dest = lax.rem(2 * (me // 2 + step * UNROLL) + uu, sp)

                @pl.when(dest != me)
                def _():
                    o_copy(lay, dest).start()
            return stat

        stat = lax.fori_loop(0, n_batch // UNROLL, group, jnp.zeros((32, d), F32))
        stat_t = jnp.transpose(jnp.concatenate([stat, jnp.zeros((d - 32, d), F32)], axis=0))
        st_send[:, 0, :] = jnp.where(lane32 < 32, stat_t[0:32], pltpu.roll(stat_t[64:96], 32, 1))

        def send_stat(i, carry):
            dest = lax.rem(me + i, sp)
            remote(st_send.at[dest // 2], st_recv.at[lay, me], st_ssem.at[lay], st_rsem.at[lay], {'sp': dest}).start()
            return carry
        lax.fori_loop(1, sp, send_stat, 0)
        mine = pl.ds(pl.multiple_of(me * 16, 16), 16)
        o_recv[lay, mine, :] = o_send[mine, :]
        st_recv[lay, me] = st_send[me // 2]
        local(kc_v.at[lay], ko_hbm.at[lay], out_sem.at[lay]).start()
        local(vc_v.at[lay], vo_hbm.at[lay], out_sem.at[2 + lay]).start()

        most = pl.ds(0, last * 16)
        remote(st_recv.at[lay, pl.ds(0, last)], st_recv.at[lay, pl.ds(0, last)], st_ssem.at[lay], st_rsem.at[lay], partner).wait_recv()
        stats = st_recv[lay, :, 0, :]
        top = jnp.max(stats, axis=0, keepdims=True)
        scale = jnp.exp(stats - top)
        denom = jnp.sum(pltpu.roll(scale, 32, 1) * stats, axis=0, keepdims=True)
        denom = pltpu.roll(jnp.broadcast_to(denom, (8, d)), d - 32, 1)
        tr_v[...] = jnp.transpose(jnp.concatenate([scale, denom, jnp.zeros((d - sp - 8, d), F32)], axis=0))
        factors = tr_v[pl.ds(pl.multiple_of(lax.rem(me, 2) * 16, 16), 16), :]
        remote(o_recv.at[lay, most], o_recv.at[lay, most], o_ssem.at[lay], o_rsem.at[lay], partner).wait_recv()
        merged = jnp.zeros((16, d), F32)
        for i in range(sp):
            merged = merged + factors[:, i:i + 1] * o_recv[lay, i * 16:i * 16 + 16, :]
        at_v[...] = merged / factors[:, sp:sp + 1]
        remote(o_send.at[most], o_send.at[most], o_ssem.at[lay], o_rsem.at[lay], partner).wait_send()
        remote(st_recv.at[lay, pl.ds(0, last)], st_recv.at[lay, pl.ds(0, last)], st_ssem.at[lay], st_rsem.at[lay], partner).wait_send()
        cols = []
        for g in range(heads):
            cols.append(jnp.concatenate([jnp.broadcast_to(at_v[g:g + 1, :], (8, d)), jnp.broadcast_to(at_v[8 + g:9 + g, :], (8, d))], axis=0))
        return jnp.concatenate(cols, axis=1).astype(BF16)

    def o_copy(lay, dest):
        return remote(o_send.at[pl.ds(pl.multiple_of(dest * 16, 16), 16)], o_recv.at[lay, pl.ds(pl.multiple_of(me * 16, 16), 16)],
                      o_ssem.at[lay], o_rsem.at[lay], {'sp': dest})

    def add_cores(i, part):
        x_send[i] = part
        copy = remote(x_send.at[i], x_recv.at[i], x_ssem.at[i], x_rsem.at[i], partner)
        copy.start()
        copy.wait()
        return part + x_recv[i]

    def mlp(lay, h):
        lane_c = iota((16, CHUNK), 1)

        def act(j):
            step = lay * n_chunks + j
            chunk_copy(step, 0).wait()
            chunk_copy(step, 1).wait()
            slot = step % SLOTS
            gate = dot(h, wg_v[slot])
            up = dot(h, wu_v[slot])
            a = gate * jax.nn.sigmoid(gate) * up
            return jnp.where(lane_c >= j * CHUNK - jnp.minimum(j * CHUNK, ff - CHUNK), a, 0.0).astype(BF16)

        def down(j, a):
            step = lay * n_chunks + j
            chunk_copy(step, 2).wait()
            return dot(a, wd_v[step % SLOTS])

        def refill(j):
            step = lay * n_chunks + j + SLOTS

            @pl.when(step < total)
            def _():
                for which in range(3):
                    chunk_copy(step, which).start()

        def body(j, a):
            nxt = act(j)
            acc_v[...] += down(j - 1, a)
            refill(j - 1)
            return nxt

        a = act(0)
        acc_v[...] = jnp.zeros_like(acc_v)
        a = lax.fori_loop(1, n_chunks, body, a)
        out = acc_v[...] + down(n_chunks - 1, a)
        refill(n_chunks - 1)
        return out

    def finish_layer(lay, u, attn):
        local(wo_hbm.at[lay], wo_v, wo_sem.at[0]).wait()
        u = rounded(u + add_cores(2 * lay, dot(attn, wo_v[...])))
        if lay == 0:
            local(wo_hbm.at[1], wo_v, wo_sem.at[0]).start()
        h = norm(u, gm_ref[pl.ds(lay, 1), :].astype(F32))
        return rounded(u + add_cores(2 * lay + 1, mlp(lay, h)))

    def send_all(send):
        def body(i, carry):
            dest = 0
            for unit in (side * side, side, 1):
                dest = dest + lax.rem(me // unit + i // unit + side // 2, side) * unit

            @pl.when(dest != me)
            def _():
                send(dest)
            return carry
        lax.fori_loop(0, sp, body, 0)

    def wait_cache(lay):
        local(kc_hbm.at[lay], kc_v.at[lay], cache_sem.at[lay]).wait()
        local(vc_hbm.at[lay], vc_v.at[lay], cache_sem.at[2 + lay]).wait()

    wait_cache(0)
    pl.semaphore_wait(barrier, sp)

    def rows0(b, ahead):
        return k0_v[pl.ds(ahead * n_batch + b, 1), :], v0_v[pl.ds(ahead * n_batch + b, 1), :]

    def rows1(b, ahead):
        chip = 2 * b + ahead // 2
        return kv_recv[chip, pl.ds(lax.rem(ahead, 2), 1), :], kv_recv[chip, pl.ds(2 + lax.rem(ahead, 2), 1), :]

    u = finish_layer(0, u, attention(0, q0_v, rows0))

    h = norm(u, ga_ref[pl.ds(1, 1), :].astype(F32))
    for copy in qkv_copies(1):
        copy.wait()
    sub = row16 % 8
    q = jnp.zeros((16, d), F32)
    for pair in range(heads // 2):
        both = dot(h, wqkv_v[:, pair * 256:pair * 256 + 256])
        q = jnp.where(sub == 2 * pair, both[:, :d], jnp.where(sub == 2 * pair + 1, both[:, d:], q))
    both = dot(h, wqkv_v[:, qw:qw + 256])
    q_send[...] = rounded(rope(q, my_cos, my_sin))
    k = rounded(rope(both[:, :d], my_cos, my_sin))
    v = rounded(both[:, d:])
    sub8 = iota((8, d), 0)
    kv = jnp.where(sub8 == 0, k[:8], jnp.where(sub8 == 1, k[8:], jnp.where(sub8 == 2, v[:8], v[8:])))
    kv_send[...] = kv[:4]
    mine = pl.ds(pl.multiple_of(me * 16, 16), 16)

    def send_qkv(dest):
        remote(kv_send, kv_recv.at[me], ag_ssem.at[1], ag_rsem.at[1], {'sp': dest}).start()
        remote(q_send, q_recv.at[mine], ag_ssem.at[0], ag_rsem.at[0], {'sp': dest}).start()
    send_all(send_qkv)
    q_recv[mine, :] = q_send[...]
    kv_recv[me] = kv_send[...]
    most = pl.ds(0, last * 16)
    wait_cache(1)
    for ref, sem in ((q_recv.at[most], 0), (kv_recv.at[pl.ds(0, last)], 1)):
        both_ways = remote(ref, ref, ag_ssem.at[sem], ag_rsem.at[sem], partner)
        both_ways.wait_recv()
        both_ways.wait_send()

    u = finish_layer(1, u, attention(1, q_recv, rows1))

    acc_v[...] = u
    half = width // 2
    msg = jnp.zeros((16, d), F32)
    for cg in range(8):
        msg = jnp.where(sub == cg, acc_v[:, pl.ds(pl.multiple_of(core * half + cg * d, d), d)], msg)
    h_send[...] = msg

    def send_hidden(dest):
        remote(h_send, h_recv.at[mine], ag_ssem.at[2], ag_rsem.at[2], {'sp': dest}).start()
    send_all(send_hidden)
    h_recv[mine, :] = h_send[...]
    both_ways = remote(h_recv.at[most], h_recv.at[most], ag_ssem.at[2], ag_rsem.at[2], partner)
    both_ways.wait_recv()
    both_ways.wait_send()
    swap = remote(h_recv, h_other, ag_ssem.at[3], ag_rsem.at[3], partner)
    swap.start()

    def spread(ref, which):
        for s in range(n_steps):
            for cg in range(8):
                rows = ref[pl.ds(s * 8 + cg, n_batch, stride=n_steps * 8), :]
                out_v[s * n_batch:(s + 1) * n_batch, pl.ds(pl.multiple_of(which * half + cg * d, d), d)] = rows.astype(BF16)
    spread(h_recv, core)
    swap.wait()
    spread(h_other, 1 - core)
    done = local(out_v, hid_hbm, in_sem.at[1])
    done.start()
    for lay in range(2):
        local(kc_v.at[lay], ko_hbm.at[lay], out_sem.at[lay]).wait()
        local(vc_v.at[lay], vo_hbm.at[lay], out_sem.at[2 + lay]).wait()
    done.wait()


def solution(mesh):
    sp = mesh.shape['sp']
    side = round(sp ** (1 / 3))

    def local_fn(tok_emb, lengths, key_cache, val_cache, gain_attn, gain_mlp, w_query, w_key, w_value, w_out, w_gate, w_up, w_down):
        n_steps, n_batch, width = tok_emb.shape
        n_layers, _, loc_len, _, d = key_cache.shape
        n_tok = n_steps * n_batch
        cache_shape = (n_layers, n_batch, loc_len, d)
        inv_freq = 1.0 / (ROPE_BASE ** (jnp.arange(d // 2).astype(F32) * 2.0 / d))
        freq = jnp.concatenate([inv_freq, inv_freq])[None, :]
        qw = w_query.shape[2]
        vmem = pltpu.VMEM
        dma = pltpu.SemaphoreType.DMA
        in_vmem = pl.BlockSpec(memory_space=pltpu.VMEM)
        in_any = pl.BlockSpec(memory_space=pl.ANY)
        outs = pl.pallas_call(
            functools.partial(kernel, sp, n_steps, n_batch, side),
            out_shape=(jax.ShapeDtypeStruct((n_tok, width), BF16), jax.ShapeDtypeStruct(cache_shape, BF16), jax.ShapeDtypeStruct(cache_shape, BF16)),
            in_specs=[pl.BlockSpec(memory_space=pltpu.SMEM)] + [in_vmem] * 3 + [in_any] * 10,
            out_specs=(in_any,) * 3,
            scratch_shapes=[
                vmem((n_tok, width), BF16), vmem((n_tok, width), BF16), vmem((width, qw + 2 * d), BF16), vmem((qw, width), BF16),
                vmem(cache_shape, BF16), vmem(cache_shape, BF16),
                vmem((SLOTS, width, CHUNK), BF16), vmem((SLOTS, width, CHUNK), BF16), vmem((SLOTS, CHUNK, width), BF16),
                vmem((sp * 16, d), F32), vmem((n_tok, d), F32), vmem((n_tok, d), F32),
                vmem((sp * 16, d), F32), vmem((sp, 4, d), F32),
                vmem((sp * 16, d), F32), vmem((2, sp * 16, d), F32), vmem((32, 1, d), F32), vmem((2, sp, 1, d), F32),
                vmem((4, 16, width), F32), vmem((4, 16, width), F32), vmem((16, width), F32),
                vmem((16, d), F32), vmem((4, d), F32), vmem((16, d), F32),
                vmem((sp * 16, d), F32), vmem((sp * 16, d), F32), vmem((n_tok, width), BF16), vmem((d, d), F32), vmem((16, d), F32),
                dma((2,)), dma((4,)), dma((4,)), dma((3,)), dma((1,)), dma((SLOTS, 3)),
                dma((2,)), dma((2,)), dma((2,)), dma((2,)), dma((4,)), dma((4,)), dma((4,)), dma((4,)),
            ],
            compiler_params=pltpu.CompilerParams(collective_id=0, has_side_effects=True, vmem_limit_bytes=67043328),
            name='decode',
        )(lengths, freq, gain_attn, gain_mlp, tok_emb.reshape(n_tok, width), key_cache.reshape(cache_shape), val_cache.reshape(cache_shape),
          w_query, w_key, w_value, w_out, w_gate, w_up, w_down)
        hidden, new_keys, new_vals = outs
        return hidden.reshape(n_steps, n_batch, width), new_keys.reshape(key_cache.shape), new_vals.reshape(val_cache.shape)

    cache_spec = P(None, 'dp', 'sp', 'tp', None)
    col_spec = P(None, None, 'tp')
    row_spec = P(None, 'tp', None)
    emb_spec = P(None, 'dp', None)
    return jax.shard_map(local_fn, mesh=mesh, in_specs=(emb_spec, P('dp'), cache_spec, cache_spec, P(), P(), col_spec, col_spec, col_spec, row_spec, col_spec, col_spec, row_spec), out_specs=(emb_spec, cache_spec, cache_spec), check_vma=False)
```

time: 1230 us -> 109 us (0.09)
  blocking collectives: 590 us -> 0 us
  waiting for transfers between devices: 446 us -> 0 us
  Pallas kernels: 0 us -> 101 us
  matrix products: 81.9 us -> 0 us
  local copies, waits for them, and re-layouts: 79.4 us -> 6.51 us
  other arithmetic: 15.6 us -> 0.59 us
  between operations: 14.6 us -> 0.65 us
    pmax x2 -> x0, blocking collectives: 590 us -> none  [local_fn(): glob_max = lax.pmax(loc_max, 'sp')]
    psum x6 -> x0, waiting for transfers between devices: 446 us -> none  [the longest x2 355 us: local_fn(): lax.psum(jnp.concatenate([loc_out, loc_sum], axis=-1) * rescale, 'sp')]
    pallas_call x0 -> x1, Pallas kernels: none -> 101 us  [local_fn(): pl.pallas_call(functools.partial(kernel, sp, n_steps, n_batch, side), out...]
    dot_general x18 -> x0, matrix products: 81.9 us -> none  [the longest x14 75.4 us: project(): return jnp.dot(normed, weight, preferred_element_type=jnp.float32)]
    scatter x4 -> x0, local copies, waits for them, and re-layouts: 45 us -> none  [the longest x2 27.6 us: local_fn(): new_vals.at[layer_idx, row_ids, write_slot]]
    dot_general x3 -> x0, local copies, waits for them, and re-layouts: 19 us -> none  [project(): return jnp.dot(normed, weight, preferred_element_type=jnp.float32)]
  transfers between devices with their start and end apart: 6 -> 0, of which waited for: 6 -> 0; matrix products, arithmetic and copies ran while one was open for 1% -> 0% of each run, Pallas kernels for 0% -> 0%
where the time goes in v1:
time: 109 us
  Pallas kernels  101 us (93%)
  local copies, waits for them, and re-layouts  6.51 us (6%)
    pallas_call x1, Pallas kernels, local_fn(): pl.pallas_call(functools.partial(kernel, sp, n_steps, n_batch, side), out...  101 us
    unnamed x5, local copies, waits for them, and re-layouts  6.51 us

profile of v1, /device:TPU:1, one launch (start us, length us, event | category | flops | bytes accessed | tf_op | source)
XLA Modules:
  0.0 109.2 jit_solution(10141733251648876097)
XLA Ops:
  0.6 0.6 maximum_bitcast_fusion.freq_ref
  1.2 101.4 %decode.1 = (bf16[128,2048]{1,0:T(8,128)(2,1)}, bf16[2,32,128,128]{3,2,1,0:T(8,128)(2,1)}, bf16[2,32,128,128]{3,2,1,0:T(8,128)(2,1)}) custom-call(s32[32]{0:T(128)} %len_ref.1, f32[1,128]{1,0:T(1,128)} %maximum_bitcast_fusion.freq_ref, bf16[2,2048]{1,0:T(2,128)(2,1)} %ga_ref.1, bf16[2,2048]{1,0:T(2,128)(2,1)} %gm_ref.1, bf16[128,2048]{1,0:T(8,128)(2,1)} %bitcast.16, ...), custom_call_target="tpu_custom_call" | custom-call | tf_op jit(solution)/shard_map/decode/pallas_call | solution.py:380
  102.7 1.9 %copy.21 = bf16[4,32,2048]{2,1,0:T(8,128)(2,1)} copy(bf16[4,32,2048]{2,1,0:T(8,128)(2,1)} %bitcast.17) | data formatting | bytes 1048576
  104.6 0.0 copy-start
  104.6 3.3 %copy.22 = bf16[2,32,128,1,128]{4,2,3,1,0:T(8,128)(2,1)} copy(bf16[2,32,128,1,128]{4,2,3,1,0:T(8,128)(2,1)} %bitcast.15) | data formatting | bytes 4194304
  107.9 0.0 copy-done
  107.9 1.3 %copy.23 = bf16[2,32,128,1,128]{4,2,3,1,0:T(8,128)(2,1)} copy(bf16[2,32,128,1,128]{4,2,3,1,0:T(8,128)(2,1)S(1)} %bitcast.14) | data formatting | bytes 4194304
  (1 shorter events, 0.0 us)
Async XLA Ops:
  104.6 3.3 %copy-start = (bf16[2,32,128,128]{3,2,1,0:T(8,128)(2,1)S(1)}, bf16[2,32,128,128]{3,2,1,0:T(8,128)(2,1)}, u32[]{:S(2)}) copy-start(bf16[2,32,128,128]{3,2,1,0:T(8,128)(2,1)} %get-tuple-element.8) | copy-start | bytes 6291460

commit v2 on v1

--- a/solution.py
+++ b/solution.py
@@ -2,6 +2,7 @@
 
 import jax
 import jax.numpy as jnp
+import numpy as np
 from jax import lax
 from jax.experimental import pallas as pl
 from jax.experimental.pallas import tpu as pltpu
@@ -10,7 +11,7 @@
 EPS = 1e-5
 ROPE_BASE = 500000.0
 CHUNK = 512
-SLOTS = 6
+SLOTS = 7
 UNROLL = 8
 F32 = jnp.float32
 BF16 = jnp.bfloat16
@@ -34,10 +35,10 @@
            len_ref, freq_ref, ga_ref, gm_ref, x_hbm, kc_hbm, vc_hbm, wq_hbm, wk_hbm, wv_hbm, wo_hbm, wg_hbm, wu_hbm, wd_hbm,
            hid_hbm, ko_hbm, vo_hbm,
            x_v, xn_v, wqkv_v, wo_v, kc_v, vc_v, wg_v, wu_v, wd_v, q0_v, k0_v, v0_v,
-           q_recv, kv_recv, o_send, o_recv, st_send, st_recv, x_send, x_recv, acc_v, q_send, kv_send, h_send,
-           h_recv, h_other, out_v, tr_v, at_v,
+           qkv_recv, o_send, o_recv, st_send, st_recv, x_send, x_recv, acc_v, qkv_send, h_send,
+           h_recv, h_other, tr_v, at_v,
            in_sem, cache_sem, out_sem, wqkv_sem, wo_sem, slot_sem,
-           o_ssem, o_rsem, st_ssem, st_rsem, x_ssem, x_rsem, ag_ssem, ag_rsem):
+           o_ssem, o_rsem, st_ssem, st_rsem, x_ssem, x_rsem, ag_ssem, qkv_rsem, h_rsem, sw_ssem, sw_rsem):
     me = lax.axis_index('sp')
     core = lax.axis_index('tp')
     n_tok = n_steps * n_batch
@@ -50,6 +51,9 @@
     total = 2 * n_chunks
     last = sp - 1
     partner = {'tp': 1 - core}
+    plane = side * side
+    my_plane = me // plane
+    out_v = x_v
 
     def local(src, dst, sem):
         return pltpu.make_async_copy(src, dst, sem)
@@ -58,9 +62,19 @@
         return pltpu.make_async_remote_copy(src_ref=src, dst_ref=dst, send_sem=ssem, recv_sem=rsem, device_id=dev, device_id_type=MESH)
 
     def qkv_copies(lay):
-        return (local(wq_hbm.at[lay], wqkv_v.at[:, pl.ds(0, qw)], wqkv_sem.at[0]),
-                local(wk_hbm.at[lay], wqkv_v.at[:, pl.ds(qw, d)], wqkv_sem.at[1]),
-                local(wv_hbm.at[lay], wqkv_v.at[:, pl.ds(qw + d, d)], wqkv_sem.at[2]))
+        copies = [local(wq_hbm.at[lay, :, pl.ds(i * 256, 256)], wqkv_v.at[:, pl.ds(i * 256, 256)], wqkv_sem.at[i]) for i in range(qw // 256)]
+        copies.append(local(wk_hbm.at[lay], wqkv_v.at[:, pl.ds(qw, d)], wqkv_sem.at[qw // 256]))
+        copies.append(local(wv_hbm.at[lay], wqkv_v.at[:, pl.ds(qw + d, d)], wqkv_sem.at[qw // 256 + 1]))
+        return copies
+
+    def each_other(send):
+        many = 9 if last % 9 == 0 else 1
+
+        def body(i, carry):
+            for j in range(many):
+                send(lax.rem(me + 1 + lax.rem(i * many + j + sp // 2 - 1, last), sp))
+            return carry
+        lax.fori_loop(0, last // many, body, 0)
 
     def chunk_copy(step, which):
         lay = step // n_chunks
@@ -76,11 +90,7 @@
     for copy in qkv_copies(0):
         copy.start()
     barrier = pltpu.get_barrier_semaphore()
-
-    def greet(i, carry):
-        pl.semaphore_signal(barrier, inc=1, device_id={'sp': lax.rem(me + i, sp)}, device_id_type=MESH)
-        return carry
-    lax.fori_loop(1, sp, greet, 0)
+    each_other(lambda dest: pl.semaphore_signal(barrier, inc=1, device_id={'sp': dest}, device_id_type=MESH))
     pl.semaphore_signal(barrier, inc=1, device_id=partner, device_id_type=MESH)
 
     lane = iota((1, d), 1)
@@ -108,8 +118,6 @@
 
     x_copy.wait()
     xn_v[...] = norm(x_v[...].astype(F32), ga_ref[pl.ds(0, 1), :].astype(F32))
-    for copy in qkv_copies(0):
-        copy.wait()
     for lay in range(2):
         local(kc_hbm.at[lay], kc_v.at[lay], cache_sem.at[lay]).start()
         local(vc_hbm.at[lay], vc_v.at[lay], cache_sem.at[2 + lay]).start()
@@ -123,13 +131,17 @@
     lax.fori_loop(0, SLOTS, prefetch, 0)
 
     xn = xn_v[...]
+    waits = qkv_copies(0)
     for pair in range(heads // 2):
+        waits[pair].wait()
         both = dot(xn, wqkv_v[:, pair * 256:pair * 256 + 256])
         for g in (2 * pair, 2 * pair + 1):
             off = (g % 2) * d
             q = rounded(rope(both[:, off:off + d], cos_t, sin_t))
             for s in range(n_steps):
                 q0_v[pl.ds(s * heads + g, n_batch, stride=n_steps * heads), :] = q[s * n_batch:(s + 1) * n_batch]
+    waits[-2].wait()
+    waits[-1].wait()
     both = dot(xn, wqkv_v[:, qw:qw + 256])
     k0_v[...] = rounded(rope(both[:, :d], cos_t, sin_t))
     v0_v[...] = rounded(both[:, d:])
@@ -144,10 +156,13 @@
     lane32 = iota((32, d), 1)
     slot_rows = iota((d, d), 0).astype(F32).astype(BF16)
 
-    def attention(lay, q_ref, new_rows):
+    def attention(lay, arrive, queries, new_rows):
         def group(step, stat):
+            first = lax.rem(my_plane + step, side) * UNROLL
+            turn = lax.rem(me, plane) // 2
+            arrive(step)
             for uu in range(UNROLL):
-                b = lax.rem(me // 2 + step * UNROLL + uu, n_batch)
+                b = first + lax.rem(turn + uu, UNROLL)
                 length = len_ref[b]
                 ahead = lax.rem(me - length + 1024 * sp, sp)
                 slot = jnp.where(ahead < n_steps, (length + ahead) // sp, -1)
@@ -158,7 +173,7 @@
                 kc_v[lay, b] = k_new
                 vc_v[lay, b] = v_new
                 rows = pl.ds(pl.multiple_of(b * 32, 32), 32)
-                q = q_ref[rows, :].astype(BF16)
+                q = queries(b).astype(BF16)
                 s = lax.dot_general(q, k_new, (((1,), (1,)), ((), ())), preferred_element_type=F32) * (d ** -0.5)
                 s = jnp.where(pos_row <= length, s, -1e30)
                 m = jnp.max(s, axis=-1, keepdims=True)
@@ -167,7 +182,7 @@
                 o_send[rows, :] = dot(w.astype(BF16), v_new)
                 stat = jnp.where(lane32 == b, m, jnp.where(lane32 == 64 + b, l, stat))
             for uu in range(2 * UNROLL):
-                dest = lax.rem(2 * (me // 2 + step * UNROLL) + uu, sp)
+                dest = 2 * first + lax.rem(2 * turn + uu, 2 * UNROLL)
 
                 @pl.when(dest != me)
                 def _():
@@ -178,11 +193,7 @@
         stat_t = jnp.transpose(jnp.concatenate([stat, jnp.zeros((d - 32, d), F32)], axis=0))
         st_send[:, 0, :] = jnp.where(lane32 < 32, stat_t[0:32], pltpu.roll(stat_t[64:96], 32, 1))
 
-        def send_stat(i, carry):
-            dest = lax.rem(me + i, sp)
-            remote(st_send.at[dest // 2], st_recv.at[lay, me], st_ssem.at[lay], st_rsem.at[lay], {'sp': dest}).start()
-            return carry
-        lax.fori_loop(1, sp, send_stat, 0)
+        each_other(lambda dest: remote(st_send.at[dest // 2], st_recv.at[lay, me], st_ssem.at[lay], st_rsem.at[lay], {'sp': dest}).start())
         mine = pl.ds(pl.multiple_of(me * 16, 16), 16)
         o_recv[lay, mine, :] = o_send[mine, :]
         st_recv[lay, me] = st_send[me // 2]
@@ -268,18 +279,6 @@
         h = norm(u, gm_ref[pl.ds(lay, 1), :].astype(F32))
         return rounded(u + add_cores(2 * lay + 1, mlp(lay, h)))
 
-    def send_all(send):
-        def body(i, carry):
-            dest = 0
-            for unit in (side * side, side, 1):
-                dest = dest + lax.rem(me // unit + i // unit + side // 2, side) * unit
-
-            @pl.when(dest != me)
-            def _():
-                send(dest)
-            return carry
-        lax.fori_loop(0, sp, body, 0)
-
     def wait_cache(lay):
         local(kc_hbm.at[lay], kc_v.at[lay], cache_sem.at[lay]).wait()
         local(vc_hbm.at[lay], vc_v.at[lay], cache_sem.at[2 + lay]).wait()
@@ -287,17 +286,36 @@
     wait_cache(0)
     pl.semaphore_wait(barrier, sp)
 
+    def queries0(b):
+        return q0_v[pl.ds(pl.multiple_of(b * 32, 32), 32), :]
+
     def rows0(b, ahead):
         return k0_v[pl.ds(ahead * n_batch + b, 1), :], v0_v[pl.ds(ahead * n_batch + b, 1), :]
 
+    def queries1(b):
+        return jnp.concatenate([qkv_recv[2 * b, 0:16, :], qkv_recv[2 * b + 1, 0:16, :]], axis=0)
+
     def rows1(b, ahead):
-        chip = 2 * b + ahead // 2
-        return kv_recv[chip, pl.ds(lax.rem(ahead, 2), 1), :], kv_recv[chip, pl.ds(2 + lax.rem(ahead, 2), 1), :]
-
-    u = finish_layer(0, u, attention(0, q0_v, rows0))
+        kv = jnp.where(ahead >= 2, qkv_recv[2 * b + 1, 16:20, :], qkv_recv[2 * b, 16:20, :])
+        odd = lax.rem(ahead, 2) == 1
+        return jnp.where(odd, kv[1:2], kv[0:1]), jnp.where(odd, kv[3:4], kv[2:3])
+
+    def wait_plane(step, part, ssem, rsem):
+        which = lax.rem(my_plane + step, side)
+
+        @pl.when(step == 0)
+        def _():
+            remote(part(plane - 1), part(plane - 1), ssem, rsem.at[which], partner).wait_recv()
+
+        @pl.when(step != 0)
+        def _():
+            remote(part(plane), part(plane), ssem, rsem.at[which], partner).wait_recv()
+
+    u = finish_layer(0, u, attention(0, lambda step: None, queries0, rows0))
 
     h = norm(u, ga_ref[pl.ds(1, 1), :].astype(F32))
-    for copy in qkv_copies(1):
+    waits = qkv_copies(1)
+    for copy in waits:
         copy.wait()
     sub = row16 % 8
     q = jnp.zeros((16, d), F32)
@@ -305,28 +323,21 @@
         both = dot(h, wqkv_v[:, pair * 256:pair * 256 + 256])
         q = jnp.where(sub == 2 * pair, both[:, :d], jnp.where(sub == 2 * pair + 1, both[:, d:], q))
     both = dot(h, wqkv_v[:, qw:qw + 256])
-    q_send[...] = rounded(rope(q, my_cos, my_sin))
+    qkv_send[0:16, :] = rounded(rope(q, my_cos, my_sin))
     k = rounded(rope(both[:, :d], my_cos, my_sin))
     v = rounded(both[:, d:])
     sub8 = iota((8, d), 0)
     kv = jnp.where(sub8 == 0, k[:8], jnp.where(sub8 == 1, k[8:], jnp.where(sub8 == 2, v[:8], v[8:])))
-    kv_send[...] = kv[:4]
-    mine = pl.ds(pl.multiple_of(me * 16, 16), 16)
-
-    def send_qkv(dest):
-        remote(kv_send, kv_recv.at[me], ag_ssem.at[1], ag_rsem.at[1], {'sp': dest}).start()
-        remote(q_send, q_recv.at[mine], ag_ssem.at[0], ag_rsem.at[0], {'sp': dest}).start()
-    send_all(send_qkv)
-    q_recv[mine, :] = q_send[...]
-    kv_recv[me] = kv_send[...]
-    most = pl.ds(0, last * 16)
+    qkv_send[16:20, :] = kv[:4]
+    each_other(lambda dest: remote(qkv_send, qkv_recv.at[me], ag_ssem.at[0], qkv_rsem.at[my_plane], {'sp': dest}).start())
+    qkv_recv[me] = qkv_send[...]
     wait_cache(1)
-    for ref, sem in ((q_recv.at[most], 0), (kv_recv.at[pl.ds(0, last)], 1)):
-        both_ways = remote(ref, ref, ag_ssem.at[sem], ag_rsem.at[sem], partner)
-        both_ways.wait_recv()
-        both_ways.wait_send()
-
-    u = finish_layer(1, u, attention(1, q_recv, rows1))
+
+    def arrive(step):
+        wait_plane(step, lambda n: qkv_recv.at[pl.ds(0, n)], ag_ssem.at[0], qkv_rsem)
+
+    u = finish_layer(1, u, attention(1, arrive, queries1, rows1))
+    remote(qkv_recv.at[pl.ds(0, last)], qkv_recv.at[pl.ds(0, last)], ag_ssem.at[0], qkv_rsem.at[0], partner).wait_send()
 
     acc_v[...] = u
     half = width // 2
@@ -335,15 +346,16 @@
         msg = jnp.where(sub == cg, acc_v[:, pl.ds(pl.multiple_of(core * half + cg * d, d), d)], msg)
     h_send[...] = msg
 
-    def send_hidden(dest):
-        remote(h_send, h_recv.at[mine], ag_ssem.at[2], ag_rsem.at[2], {'sp': dest}).start()
-    send_all(send_hidden)
+    mine = pl.ds(pl.multiple_of(me * 16, 16), 16)
+    each_other(lambda dest: remote(h_send, h_recv.at[mine], ag_ssem.at[1], h_rsem.at[my_plane], {'sp': dest}).start())
     h_recv[mine, :] = h_send[...]
-    both_ways = remote(h_recv.at[most], h_recv.at[most], ag_ssem.at[2], ag_rsem.at[2], partner)
-    both_ways.wait_recv()
-    both_ways.wait_send()
-    swap = remote(h_recv, h_other, ag_ssem.at[3], ag_rsem.at[3], partner)
-    swap.start()
+
+    def swap(step):
+        rows = pl.ds(pl.multiple_of(lax.rem(my_plane + step, side) * plane * 16, plane * 16), plane * 16)
+        return remote(h_recv.at[rows], h_other.at[rows], sw_ssem.at[step], sw_rsem.at[step], partner)
+    for step in range(side):
+        wait_plane(step, lambda n: h_recv.at[pl.ds(0, n * 16)], ag_ssem.at[1], h_rsem)
+        swap(step).start()
 
     def spread(ref, which):
         for s in range(n_steps):
@@ -351,14 +363,51 @@
                 rows = ref[pl.ds(s * 8 + cg, n_batch, stride=n_steps * 8), :]
                 out_v[s * n_batch:(s + 1) * n_batch, pl.ds(pl.multiple_of(which * half + cg * d, d), d)] = rows.astype(BF16)
     spread(h_recv, core)
-    swap.wait()
+    for step in range(side):
+        swap(step).wait()
     spread(h_other, 1 - core)
     done = local(out_v, hid_hbm, in_sem.at[1])
     done.start()
+    most = pl.ds(0, last * 16)
+    remote(h_recv.at[most], h_recv.at[most], ag_ssem.at[1], h_rsem.at[0], partner).wait_send()
     for lay in range(2):
         local(kc_v.at[lay], ko_hbm.at[lay], out_sem.at[lay]).wait()
         local(vc_v.at[lay], vo_hbm.at[lay], out_sem.at[2 + lay]).wait()
     done.wait()
+
+
+def deliver_kernel(parts, *refs):
+    n = len(parts)
+    srcs, dsts, bufs, sems = refs[:n], refs[n:2 * n], refs[2 * n:3 * n], refs[3 * n]
+    loads, stores = [], []
+    for i, part in enumerate(parts):
+        for j in range(srcs[i].shape[0] // part):
+            rows = pl.ds(j * part, part)
+            loads.append(pltpu.make_async_copy(srcs[i].at[rows], bufs[i].at[rows], sems.at[0, len(loads)]))
+            stores.append(pltpu.make_async_copy(bufs[i].at[rows], dsts[i].at[rows], sems.at[1, len(stores)]))
+    for load in loads:
+        load.start()
+    for load, store in zip(loads, stores):
+        load.wait()
+        store.start()
+    for store in stores:
+        store.wait()
+
+
+def deliver(arrays):
+    flat = [a.reshape(-1, a.shape[-1]) for a in arrays]
+    parts = [max(a.shape[0] // 4, 16) if a.shape[0] > 1024 else a.shape[0] for a in flat]
+    count = sum(a.shape[0] // part for a, part in zip(flat, parts))
+    any_space = pl.BlockSpec(memory_space=pl.ANY)
+    return pl.pallas_call(
+        functools.partial(deliver_kernel, parts),
+        out_shape=tuple(jax.ShapeDtypeStruct(a.shape, a.dtype) for a in flat),
+        in_specs=[any_space] * len(flat),
+        out_specs=(any_space,) * len(flat),
+        scratch_shapes=[pltpu.VMEM(a.shape, a.dtype) for a in flat] + [pltpu.SemaphoreType.DMA((2, count))],
+        compiler_params=pltpu.CompilerParams(vmem_limit_bytes=67043328),
+        name='deliver',
+    )(*flat)
 
 
 def solution(mesh):
@@ -370,8 +419,8 @@
         n_layers, _, loc_len, _, d = key_cache.shape
         n_tok = n_steps * n_batch
         cache_shape = (n_layers, n_batch, loc_len, d)
-        inv_freq = 1.0 / (ROPE_BASE ** (jnp.arange(d // 2).astype(F32) * 2.0 / d))
-        freq = jnp.concatenate([inv_freq, inv_freq])[None, :]
+        inv_freq = np.float32(1.0) / np.float32(ROPE_BASE) ** (np.arange(d // 2, dtype=np.float32) * np.float32(2.0) / np.float32(d))
+        freq = jnp.asarray(np.concatenate([inv_freq, inv_freq])[None, :], F32)
         qw = w_query.shape[2]
         vmem = pltpu.VMEM
         dma = pltpu.SemaphoreType.DMA
@@ -387,19 +436,19 @@
                 vmem(cache_shape, BF16), vmem(cache_shape, BF16),
                 vmem((SLOTS, width, CHUNK), BF16), vmem((SLOTS, width, CHUNK), BF16), vmem((SLOTS, CHUNK, width), BF16),
                 vmem((sp * 16, d), F32), vmem((n_tok, d), F32), vmem((n_tok, d), F32),
-                vmem((sp * 16, d), F32), vmem((sp, 4, d), F32),
+                vmem((sp, 20, d), F32),
                 vmem((sp * 16, d), F32), vmem((2, sp * 16, d), F32), vmem((32, 1, d), F32), vmem((2, sp, 1, d), F32),
                 vmem((4, 16, width), F32), vmem((4, 16, width), F32), vmem((16, width), F32),
-                vmem((16, d), F32), vmem((4, d), F32), vmem((16, d), F32),
-                vmem((sp * 16, d), F32), vmem((sp * 16, d), F32), vmem((n_tok, width), BF16), vmem((d, d), F32), vmem((16, d), F32),
-                dma((2,)), dma((4,)), dma((4,)), dma((3,)), dma((1,)), dma((SLOTS, 3)),
-                dma((2,)), dma((2,)), dma((2,)), dma((2,)), dma((4,)), dma((4,)), dma((4,)), dma((4,)),
+                vmem((20, d), F32), vmem((16, d), F32),
+                vmem((sp * 16, d), F32), vmem((sp * 16, d), F32), vmem((d, d), F32), vmem((16, d), F32),
+                dma((2,)), dma((4,)), dma((4,)), dma((qw // 256 + 2,)), dma((1,)), dma((SLOTS, 3)),
+                dma((2,)), dma((2,)), dma((2,)), dma((2,)), dma((4,)), dma((4,)), dma((2,)), dma((side,)), dma((side,)), dma((side,)), dma((side,)),
             ],
             compiler_params=pltpu.CompilerParams(collective_id=0, has_side_effects=True, vmem_limit_bytes=67043328),
             name='decode',
         )(lengths, freq, gain_attn, gain_mlp, tok_emb.reshape(n_tok, width), key_cache.reshape(cache_shape), val_cache.reshape(cache_shape),
           w_query, w_key, w_value, w_out, w_gate, w_up, w_down)
-        hidden, new_keys, new_vals = outs
+        hidden, new_keys, new_vals = deliver(outs)
         return hidden.reshape(n_steps, n_batch, width), new_keys.reshape(key_cache.shape), new_vals.reshape(val_cache.shape)
 
     cache_spec = P(None, 'dp', 'sp', 'tp', None)

time: 109 us -> 102 us (0.936)
  local copies, waits for them, and re-layouts: 6.51 us -> 0 us
    unnamed x5 -> x0, local copies, waits for them, and re-layouts: 6.51 us -> none
    pallas_call x1, Pallas kernels: 101 us -> 97 us  [local_fn(): pl.pallas_call(functools.partial(kernel, sp, n_steps, n_batch, side), out...]
    pallas_call x0 -> x1, Pallas kernels: none -> 4.16 us  [deliver(): pl.pallas_call(functools.partial(deliver_kernel, parts), out_shape=tuple(...]
where the time goes in v2:
time: 102 us
  Pallas kernels  101 us (99%)
    pallas_call x1, Pallas kernels, local_fn(): pl.pallas_call(functools.partial(kernel, sp, n_steps, n_batch, side), out...  97 us
    pallas_call x1, Pallas kernels, deliver(): pl.pallas_call(functools.partial(deliver_kernel, parts), out_shape=tuple(...  4.16 us

profile of v2, /device:TPU:1, one launch (start us, length us, event | category | flops | bytes accessed | tf_op | source)
XLA Modules:
  0.0 101.8 jit_solution(2195501783123188769)
XLA Ops:
  0.6 97.0 %decode.1 = (bf16[128,2048]{1,0:T(8,128)(2,1)}, bf16[2,32,128,128]{3,2,1,0:T(8,128)(2,1)}, bf16[2,32,128,128]{3,2,1,0:T(8,128)(2,1)}) custom-call(s32[32]{0:T(128)} %len_ref.1, f32[1,128]{1,0:T(1,128)} %constant.2.clone.freq_ref, bf16[2,2048]{1,0:T(2,128)(2,1)} %ga_ref.1, bf16[2,2048]{1,0:T(2,128)(2,1)} %gm_ref.1, bf16[128,2048]{1,0:T(8,128)(2,1)} %bitcast.16, ...), custom_call_target="tpu_custom_call" | custom-call | tf_op jit(solution)/shard_map/decode/pallas_call | solution.py:429
  97.6 4.2 %deliver.1 = (bf16[128,2048]{1,0:T(8,128)(2,1)}, bf16[8192,128]{1,0:T(8,128)(2,1)}, bf16[8192,128]{1,0:T(8,128)(2,1)}) custom-call(bf16[128,2048]{1,0:T(8,128)(2,1)} %get-tuple-element.9.refs_0_, bf16[8192,128]{1,0:T(8,128)(2,1)} %bitcast.14, bf16[8192,128]{1,0:T(8,128)(2,1)} %bitcast.15), custom_call_target="tpu_custom_call" | custom-call | tf_op jit(solution)/shard_map/deliver/pallas_call | solution.py:402

commit v3 on v2

--- a/solution.py
+++ b/solution.py
@@ -10,8 +10,8 @@
 
 EPS = 1e-5
 ROPE_BASE = 500000.0
-CHUNK = 512
-SLOTS = 7
+TEAM = 4
+PIECE = 512
 UNROLL = 8
 F32 = jnp.float32
 BF16 = jnp.bfloat16
@@ -35,10 +35,10 @@
            len_ref, freq_ref, ga_ref, gm_ref, x_hbm, kc_hbm, vc_hbm, wq_hbm, wk_hbm, wv_hbm, wo_hbm, wg_hbm, wu_hbm, wd_hbm,
            hid_hbm, ko_hbm, vo_hbm,
            x_v, xn_v, wqkv_v, wo_v, kc_v, vc_v, wg_v, wu_v, wd_v, q0_v, k0_v, v0_v,
-           qkv_recv, o_send, o_recv, st_send, st_recv, x_send, x_recv, acc_v, qkv_send, h_send,
+           qkv_recv, o_send, o_recv, st_send, st_recv, a_send, a_recv, b_send, b_recv, rows_v, res_v, qkv_send, h_send,
            h_recv, h_other, tr_v, at_v,
-           in_sem, cache_sem, out_sem, wqkv_sem, wo_sem, slot_sem,
-           o_ssem, o_rsem, st_ssem, st_rsem, x_ssem, x_rsem, ag_ssem, qkv_rsem, h_rsem, sw_ssem, sw_rsem):
+           in_sem, cache_sem, out_sem, wqkv_sem, wo_sem, mlp_sem,
+           o_ssem, o_rsem, st_ssem, st_rsem, a_ssem, a_rsem, b_ssem, b_rsem, ag_ssem, qkv_rsem, h_rsem, sw_ssem, sw_rsem):
     me = lax.axis_index('sp')
     core = lax.axis_index('tp')
     n_tok = n_steps * n_batch
@@ -47,8 +47,12 @@
     ff = wg_hbm.shape[2]
     heads = wq_hbm.shape[2] // d
     qw = heads * d
-    n_chunks = -(-ff // CHUNK)
-    total = 2 * n_chunks
+    share = wg_v.shape[2]
+    team = me // TEAM * TEAM
+    rank = lax.rem(me, TEAM)
+    col = pl.multiple_of(jnp.minimum(rank * share, ff - share), d)
+    groups = width // d
+    mine32 = 2 * groups
     last = sp - 1
     partner = {'tp': 1 - core}
     plane = side * side
@@ -76,14 +80,10 @@
             return carry
         lax.fori_loop(0, last // many, body, 0)
 
-    def chunk_copy(step, which):
-        lay = step // n_chunks
-        col = pl.multiple_of(jnp.minimum((step % n_chunks) * CHUNK, ff - CHUNK), d)
-        slot = step % SLOTS
-        if which == 2:
-            return local(wd_hbm.at[lay, pl.ds(col, CHUNK), :], wd_v.at[slot], slot_sem.at[slot, 2])
-        src, dst = ((wg_hbm, wg_v), (wu_hbm, wu_v))[which]
-        return local(src.at[lay, :, pl.ds(col, CHUNK)], dst.at[slot], slot_sem.at[slot, which])
+    def mlp_copies(lay):
+        return (local(wg_hbm.at[lay, :, pl.ds(col, share)], wg_v.at[lay], mlp_sem.at[lay, 0]),
+                local(wu_hbm.at[lay, :, pl.ds(col, share)], wu_v.at[lay], mlp_sem.at[lay, 1]),
+                local(wd_hbm.at[lay, pl.ds(col, share), :], wd_v.at[lay], mlp_sem.at[lay, 2]))
 
     x_copy = local(x_hbm, x_v, in_sem.at[0])
     x_copy.start()
@@ -91,7 +91,8 @@
         copy.start()
     barrier = pltpu.get_barrier_semaphore()
     each_other(lambda dest: pl.semaphore_signal(barrier, inc=1, device_id={'sp': dest}, device_id_type=MESH))
-    pl.semaphore_signal(barrier, inc=1, device_id=partner, device_id_type=MESH)
+    for j in range(TEAM):
+        pl.semaphore_signal(barrier, inc=1, device_id={'sp': team + j, 'tp': 1 - core}, device_id_type=MESH)
 
     lane = iota((1, d), 1)
     sign = jnp.where(lane < d // 2, -1.0, 1.0).astype(F32)
@@ -124,11 +125,9 @@
     wo_copy = local(wo_hbm.at[0], wo_v, wo_sem.at[0])
     wo_copy.start()
 
-    def prefetch(step, carry):
-        for which in range(3):
-            chunk_copy(step, which).start()
-        return carry
-    lax.fori_loop(0, SLOTS, prefetch, 0)
+    for lay in range(2):
+        for copy in mlp_copies(lay):
+            copy.start()
 
     xn = xn_v[...]
     waits = qkv_copies(0)
@@ -225,66 +224,90 @@
         return remote(o_send.at[pl.ds(pl.multiple_of(dest * 16, 16), 16)], o_recv.at[lay, pl.ds(pl.multiple_of(me * 16, 16), 16)],
                       o_ssem.at[lay], o_rsem.at[lay], {'sp': dest})
 
-    def add_cores(i, part):
-        x_send[i] = part
-        copy = remote(x_send.at[i], x_recv.at[i], x_ssem.at[i], x_rsem.at[i], partner)
-        copy.start()
-        copy.wait()
-        return part + x_recv[i]
-
-    def mlp(lay, h):
-        lane_c = iota((16, CHUNK), 1)
-
-        def act(j):
-            step = lay * n_chunks + j
-            chunk_copy(step, 0).wait()
-            chunk_copy(step, 1).wait()
-            slot = step % SLOTS
-            gate = dot(h, wg_v[slot])
-            up = dot(h, wu_v[slot])
-            a = gate * jax.nn.sigmoid(gate) * up
-            return jnp.where(lane_c >= j * CHUNK - jnp.minimum(j * CHUNK, ff - CHUNK), a, 0.0).astype(BF16)
-
-        def down(j, a):
-            step = lay * n_chunks + j
-            chunk_copy(step, 2).wait()
-            return dot(a, wd_v[step % SLOTS])
-
-        def refill(j):
-            step = lay * n_chunks + j + SLOTS
-
-            @pl.when(step < total)
-            def _():
-                for which in range(3):
-                    chunk_copy(step, which).start()
-
-        def body(j, a):
-            nxt = act(j)
-            acc_v[...] += down(j - 1, a)
-            refill(j - 1)
-            return nxt
-
-        a = act(0)
-        acc_v[...] = jnp.zeros_like(acc_v)
-        a = lax.fori_loop(1, n_chunks, body, a)
-        out = acc_v[...] + down(n_chunks - 1, a)
-        refill(n_chunks - 1)
-        return out
+    def team_exchange(send, recv, ssem, rsem, part, slots):
+        for j in range(TEAM):
+            for c in range(2):
+                @pl.when(jnp.logical_or(team + j != me, core != c))
+                def _():
+                    remote(part(j), recv.at[rank * 2 + core], ssem, rsem, {'sp': team + j, 'tp': c}).start()
+
+        recv[rank * 2 + core] = slots
+        others = remote(recv.at[pl.ds(0, 2 * TEAM - 1)], recv.at[pl.ds(0, 2 * TEAM - 1)], ssem, rsem, partner)
+        others.wait_recv()
+        others.wait_send()
+
+    sub8 = iota((8, d), 0)
+
+    def to_dense(rows):
+        out = []
+        for tok in range(2):
+            for top in range(0, groups, 8):
+                block = jnp.zeros((8, d), F32)
+                for g in range(8):
+                    block = jnp.where(sub8 == g, rows[tok * 8:tok * 8 + 8, (top + g) * d:(top + g + 1) * d], block)
+                out.append(block)
+        return jnp.concatenate(out, axis=0)
+
+    def from_dense(dense):
+        res_v[...] = dense
+        cols = []
+        for g in range(groups):
+            cols.append(jnp.concatenate([jnp.broadcast_to(res_v[g:g + 1, :], (8, d)), jnp.broadcast_to(res_v[groups + g:groups + g + 1, :], (8, d))], axis=0))
+        return jnp.concatenate(cols, axis=1)
 
     def finish_layer(lay, u, attn):
         local(wo_hbm.at[lay], wo_v, wo_sem.at[0]).wait()
-        u = rounded(u + add_cores(2 * lay, dot(attn, wo_v[...])))
+        part = dot(attn, wo_v[...]) + jnp.where(core == 0, u, 0.0)
         if lay == 0:
             local(wo_hbm.at[1], wo_v, wo_sem.at[0]).start()
-        h = norm(u, gm_ref[pl.ds(lay, 1), :].astype(F32))
-        return rounded(u + add_cores(2 * lay + 1, mlp(lay, h)))
+        dense = to_dense(part)
+        a_send[lay] = dense
+        team_exchange(a_send.at[lay], a_recv.at[lay], a_ssem.at[lay], a_rsem.at[lay], lambda j: a_send.at[lay], dense)
+        gain = gm_ref[pl.ds(lay, 1), :].astype(F32)
+        blocks = []
+        for top in range(0, groups, 8):
+            block = jnp.zeros((8, d), F32)
+            for g in range(8):
+                block = jnp.where(sub8 == g, gain[:, (top + g) * d:(top + g + 1) * d], block)
+            blocks.append(block)
+        gain = jnp.concatenate(blocks, axis=0)
+        for j in range(TEAM):
+            both = rounded(a_recv[lay, 2 * j] + a_recv[lay, 2 * j + 1])
+            for tok in range(2):
+                v = both[tok * groups:(tok + 1) * groups]
+                mean = jnp.sum(jnp.sum(v * v, axis=1, keepdims=True), axis=0, keepdims=True) / width
+                at = (2 * j + tok) * groups
+                rows_v[at:at + groups, :] = v * lax.rsqrt(mean + EPS) * gain
+        h = jnp.concatenate([rows_v[pl.ds(g, 2 * TEAM, stride=groups), :] for g in range(groups)], axis=1)
+        h = jnp.concatenate([h, h], axis=0).astype(BF16)
+        for copy in mlp_copies(lay):
+            copy.wait()
+        acts = []
+        for at in range(0, share, PIECE):
+            size = min(PIECE, share - at)
+            gate = dot(h, wg_v[lay, :, at:at + size])
+            up = dot(h, wu_v[lay, :, at:at + size])
+            keep = iota((16, size), 1) >= rank * share - col - at
+            acts.append(jnp.where(keep, gate * jax.nn.sigmoid(gate) * up, 0.0).astype(BF16))
+        down = dot(jnp.concatenate(acts, axis=1), wd_v[lay])
+        for g in range(groups):
+            b_send[lay, pl.ds(g, 2 * TEAM, stride=groups), :] = down[0:8, g * d:(g + 1) * d]
+
+        def rows_of(j):
+            return pl.ds(pl.multiple_of(j * mine32, mine32), mine32)
+        team_exchange(b_send.at[lay], b_recv.at[lay], b_ssem.at[lay], b_rsem.at[lay], lambda j: b_send.at[lay, rows_of(j)], b_send[lay, rows_of(rank), :])
+        total = b_recv[lay, 0]
+        for i in range(1, 2 * TEAM):
+            total = total + b_recv[lay, i]
+        mine = rounded(a_recv[lay, 2 * rank] + a_recv[lay, 2 * rank + 1])
+        return rounded(mine + total)
 
     def wait_cache(lay):
         local(kc_hbm.at[lay], kc_v.at[lay], cache_sem.at[lay]).wait()
         local(vc_hbm.at[lay], vc_v.at[lay], cache_sem.at[2 + lay]).wait()
 
     wait_cache(0)
-    pl.semaphore_wait(barrier, sp)
+    pl.semaphore_wait(barrier, last + TEAM)
 
     def queries0(b):
         return q0_v[pl.ds(pl.multiple_of(b * 32, 32), 32), :]
@@ -311,7 +334,7 @@
         def _():
             remote(part(plane), part(plane), ssem, rsem.at[which], partner).wait_recv()
 
-    u = finish_layer(0, u, attention(0, lambda step: None, queries0, rows0))
+    u = from_dense(finish_layer(0, u, attention(0, lambda step: None, queries0, rows0)))
 
     h = norm(u, ga_ref[pl.ds(1, 1), :].astype(F32))
     waits = qkv_copies(1)
@@ -326,7 +349,6 @@
     qkv_send[0:16, :] = rounded(rope(q, my_cos, my_sin))
     k = rounded(rope(both[:, :d], my_cos, my_sin))
     v = rounded(both[:, d:])
-    sub8 = iota((8, d), 0)
     kv = jnp.where(sub8 == 0, k[:8], jnp.where(sub8 == 1, k[8:], jnp.where(sub8 == 2, v[:8], v[8:])))
     qkv_send[16:20, :] = kv[:4]
     each_other(lambda dest: remote(qkv_send, qkv_recv.at[me], ag_ssem.at[0], qkv_rsem.at[my_plane], {'sp': dest}).start())
@@ -339,11 +361,9 @@
     u = finish_layer(1, u, attention(1, arrive, queries1, rows1))
     remote(qkv_recv.at[pl.ds(0, last)], qkv_recv.at[pl.ds(0, last)], ag_ssem.at[0], qkv_rsem.at[0], partner).wait_send()
 
-    acc_v[...] = u
     half = width // 2
-    msg = jnp.zeros((16, d), F32)
-    for cg in range(8):
-        msg = jnp.where(sub == cg, acc_v[:, pl.ds(pl.multiple_of(core * half + cg * d, d), d)], msg)
+    res_v[...] = u
+    msg = jnp.concatenate([res_v[pl.ds(pl.multiple_of(tok * groups + core * 8, 8), 8), :] for tok in range(2)], axis=0)
     h_send[...] = msg
 
     mine = pl.ds(pl.multiple_of(me * 16, 16), 16)
@@ -422,6 +442,8 @@
         inv_freq = np.float32(1.0) / np.float32(ROPE_BASE) ** (np.arange(d // 2, dtype=np.float32) * np.float32(2.0) / np.float32(d))
         freq = jnp.asarray(np.concatenate([inv_freq, inv_freq])[None, :], F32)
         qw = w_query.shape[2]
+        rows = 2 * width // d
+        share = -(-w_gate.shape[2] // (d * TEAM)) * d
         vmem = pltpu.VMEM
         dma = pltpu.SemaphoreType.DMA
         in_vmem = pl.BlockSpec(memory_space=pltpu.VMEM)
@@ -434,15 +456,16 @@
             scratch_shapes=[
                 vmem((n_tok, width), BF16), vmem((n_tok, width), BF16), vmem((width, qw + 2 * d), BF16), vmem((qw, width), BF16),
                 vmem(cache_shape, BF16), vmem(cache_shape, BF16),
-                vmem((SLOTS, width, CHUNK), BF16), vmem((SLOTS, width, CHUNK), BF16), vmem((SLOTS, CHUNK, width), BF16),
+                vmem((2, width, share), BF16), vmem((2, width, share), BF16), vmem((2, share, width), BF16),
                 vmem((sp * 16, d), F32), vmem((n_tok, d), F32), vmem((n_tok, d), F32),
                 vmem((sp, 20, d), F32),
                 vmem((sp * 16, d), F32), vmem((2, sp * 16, d), F32), vmem((32, 1, d), F32), vmem((2, sp, 1, d), F32),
-                vmem((4, 16, width), F32), vmem((4, 16, width), F32), vmem((16, width), F32),
+                vmem((2, rows, d), F32), vmem((2, 2 * TEAM, rows, d), F32), vmem((2, TEAM * rows, d), F32), vmem((2, 2 * TEAM, rows, d), F32),
+                vmem((TEAM * rows, d), F32), vmem((rows, d), F32),
                 vmem((20, d), F32), vmem((16, d), F32),
                 vmem((sp * 16, d), F32), vmem((sp * 16, d), F32), vmem((d, d), F32), vmem((16, d), F32),
-                dma((2,)), dma((4,)), dma((4,)), dma((qw // 256 + 2,)), dma((1,)), dma((SLOTS, 3)),
-                dma((2,)), dma((2,)), dma((2,)), dma((2,)), dma((4,)), dma((4,)), dma((2,)), dma((side,)), dma((side,)), dma((side,)), dma((side,)),
+                dma((2,)), dma((4,)), dma((4,)), dma((qw // 256 + 2,)), dma((1,)), dma((2, 3)),
+                dma((2,)), dma((2,)), dma((2,)), dma((2,)), dma((2,)), dma((2,)), dma((2,)), dma((2,)), dma((2,)), dma((side,)), dma((side,)), dma((side,)), dma((side,)),
             ],
             compiler_params=pltpu.CompilerParams(collective_id=0, has_side_effects=True, vmem_limit_bytes=67043328),
             name='decode',

time: 102 us -> 97.7 us (0.958)
  Pallas kernels: 101 us -> 96.9 us
    pallas_call x1, Pallas kernels: 97 us -> 92.7 us  [local_fn(): pl.pallas_call(functools.partial(kernel, sp, n_steps, n_batch, side), out...]
where the time goes in v3:
time: 97.7 us; the launch traced here: 97.5 us
  Pallas kernels  96.9 us (99%)
    pallas_call x1, Pallas kernels, local_fn(): pl.pallas_call(functools.partial(kernel, sp, n_steps, n_batch, side), out...  92.7 us
    pallas_call x1, Pallas kernels, deliver(): pl.pallas_call(functools.partial(deliver_kernel, parts), out_shape=tuple(...  4.16 us

profile of v3, /device:TPU:1, one launch (start us, length us, event | category | flops | bytes accessed | tf_op | source)
XLA Modules:
  0.0 97.5 jit_solution(7875165571112374146)
XLA Ops:
  0.6 92.7 %decode.1 = (bf16[128,2048]{1,0:T(8,128)(2,1)}, bf16[2,32,128,128]{3,2,1,0:T(8,128)(2,1)}, bf16[2,32,128,128]{3,2,1,0:T(8,128)(2,1)}) custom-call(s32[32]{0:T(128)} %len_ref.1, f32[1,128]{1,0:T(1,128)} %constant.2.clone.freq_ref, bf16[2,2048]{1,0:T(2,128)(2,1)} %ga_ref.1, bf16[2,2048]{1,0:T(2,128)(2,1)} %gm_ref.1, bf16[128,2048]{1,0:T(8,128)(2,1)} %bitcast.16, ...), custom_call_target="tpu_custom_call" | custom-call | tf_op jit(solution)/shard_map/decode/pallas_call | solution.py:451
  93.4 4.2 %deliver.1 = (bf16[128,2048]{1,0:T(8,128)(2,1)}, bf16[8192,128]{1,0:T(8,128)(2,1)}, bf16[8192,128]{1,0:T(8,128)(2,1)}) custom-call(bf16[128,2048]{1,0:T(8,128)(2,1)} %get-tuple-element.9.refs_0_, bf16[8192,128]{1,0:T(8,128)(2,1)} %bitcast.14, bf16[8192,128]{1,0:T(8,128)(2,1)} %bitcast.15), custom_call_target="tpu_custom_call" | custom-call | tf_op jit(solution)/shard_map/deliver/pallas_call | solution.py:422

commit v4 on v3

--- a/solution.py
+++ b/solution.py
@@ -85,10 +85,15 @@
                 local(wu_hbm.at[lay, :, pl.ds(col, share)], wu_v.at[lay], mlp_sem.at[lay, 1]),
                 local(wd_hbm.at[lay, pl.ds(col, share), :], wd_v.at[lay], mlp_sem.at[lay, 2]))
 
+    def start_cache(lay):
+        local(kc_hbm.at[lay], kc_v.at[lay], cache_sem.at[lay]).start()
+        local(vc_hbm.at[lay], vc_v.at[lay], cache_sem.at[2 + lay]).start()
+
     x_copy = local(x_hbm, x_v, in_sem.at[0])
     x_copy.start()
     for copy in qkv_copies(0):
         copy.start()
+    start_cache(0)
     barrier = pltpu.get_barrier_semaphore()
     each_other(lambda dest: pl.semaphore_signal(barrier, inc=1, device_id={'sp': dest}, device_id_type=MESH))
     for j in range(TEAM):
@@ -119,16 +124,6 @@
 
     x_copy.wait()
     xn_v[...] = norm(x_v[...].astype(F32), ga_ref[pl.ds(0, 1), :].astype(F32))
-    for lay in range(2):
-        local(kc_hbm.at[lay], kc_v.at[lay], cache_sem.at[lay]).start()
-        local(vc_hbm.at[lay], vc_v.at[lay], cache_sem.at[2 + lay]).start()
-    wo_copy = local(wo_hbm.at[0], wo_v, wo_sem.at[0])
-    wo_copy.start()
-
-    for lay in range(2):
-        for copy in mlp_copies(lay):
-            copy.start()
-
     xn = xn_v[...]
     waits = qkv_copies(0)
     for pair in range(heads // 2):
@@ -144,9 +139,6 @@
     both = dot(xn, wqkv_v[:, qw:qw + 256])
     k0_v[...] = rounded(rope(both[:, :d], cos_t, sin_t))
     v0_v[...] = rounded(both[:, d:])
-    for copy in qkv_copies(1):
-        copy.start()
-
     own_row = (2 * lax.rem(me, 2) + iota((16, n_tok), 0) // 8) * n_batch + me // 2
     pick = jnp.where(iota((16, n_tok), 1) == own_row, 1.0, 0.0).astype(BF16)
     u = dot(pick, x_v[...])
@@ -282,6 +274,9 @@
         h = jnp.concatenate([h, h], axis=0).astype(BF16)
         for copy in mlp_copies(lay):
             copy.wait()
+        if lay == 0:
+            for copy in mlp_copies(1):
+                copy.start()
         acts = []
         for at in range(0, share, PIECE):
             size = min(PIECE, share - at)
@@ -307,6 +302,13 @@
         local(vc_hbm.at[lay], vc_v.at[lay], cache_sem.at[2 + lay]).wait()
 
     wait_cache(0)
+
+    local(wo_hbm.at[0], wo_v, wo_sem.at[0]).start()
+    for copy in mlp_copies(0):
+        copy.start()
+    for copy in qkv_copies(1):
+        copy.start()
+    start_cache(1)
     pl.semaphore_wait(barrier, last + TEAM)
 
     def queries0(b):

time: 97.7 us -> 94.3 us (0.965)
  Pallas kernels: 96.9 us -> 93.5 us
    pallas_call x1, Pallas kernels: 92.7 us -> 89.3 us  [local_fn(): pl.pallas_call(functools.partial(kernel, sp, n_steps, n_batch, side), out...]
where the time goes in v4:
time: 94.3 us; the launch traced here: 94.1 us
  Pallas kernels  93.5 us (99%)
    pallas_call x1, Pallas kernels, local_fn(): pl.pallas_call(functools.partial(kernel, sp, n_steps, n_batch, side), out...  89.3 us
    pallas_call x1, Pallas kernels, deliver(): pl.pallas_call(functools.partial(deliver_kernel, parts), out_shape=tuple(...  4.16 us

profile of v4, /device:TPU:1, one launch (start us, length us, event | category | flops | bytes accessed | tf_op | source)
XLA Modules:
  0.0 94.1 jit_solution(5741344883111368425)
XLA Ops:
  0.6 89.3 %decode.1 = (bf16[128,2048]{1,0:T(8,128)(2,1)}, bf16[2,32,128,128]{3,2,1,0:T(8,128)(2,1)}, bf16[2,32,128,128]{3,2,1,0:T(8,128)(2,1)}) custom-call(s32[32]{0:T(128)} %len_ref.1, f32[1,128]{1,0:T(1,128)} %constant.2.clone.freq_ref, bf16[2,2048]{1,0:T(2,128)(2,1)} %ga_ref.1, bf16[2,2048]{1,0:T(2,128)(2,1)} %gm_ref.1, bf16[128,2048]{1,0:T(8,128)(2,1)} %bitcast.16, ...), custom_call_target="tpu_custom_call" | custom-call | tf_op jit(solution)/shard_map/decode/pallas_call | solution.py:453
  90.0 4.2 %deliver.1 = (bf16[128,2048]{1,0:T(8,128)(2,1)}, bf16[8192,128]{1,0:T(8,128)(2,1)}, bf16[8192,128]{1,0:T(8,128)(2,1)}) custom-call(bf16[128,2048]{1,0:T(8,128)(2,1)} %get-tuple-element.9.refs_0_, bf16[8192,128]{1,0:T(8,128)(2,1)} %bitcast.14, bf16[8192,128]{1,0:T(8,128)(2,1)} %bitcast.15), custom_call_target="tpu_custom_call" | custom-call | tf_op jit(solution)/shard_map/deliver/pallas_call | solution.py:424
